TPU v7x, 32 devices: a whole 2x2x4 slice. The times are simulated.
32 devices in a mesh: shift: 2 (over x), batch: 4 (over z), cols: 4 (over y, core).
Axes of the slice: x: 2, y: 2, z: 4, core: 2. Of those that a mesh axis runs over, the one named last changes fastest.
Arguments:
- partial_up: float32 [8, 768, 3072], P(('shift', 'batch'), None, 'cols'), parts along dimension 0, may hold values from -0.875 to 0.875
- partial_down: float32 [8, 3072, 768], P(('shift', 'batch'), 'cols'), parts along dimension 0, may hold values from -0.875 to 0.875
- partial_norm: float32 [8, 768], P(('shift', 'batch')), parts along dimension 0, may hold values from -8 to 8
- partial_bias: float32 [8, 768], P(('shift', 'batch')), parts along dimension 0, may hold values from -8 to 8
- master_up: float32 [1536, 3072], P(('shift', 'batch'), 'cols'), parts along dimension 0, may hold values from -0.21875 to 0.21875
- master_down: float32 [6144, 768], P(('shift', 'cols'), 'batch'), parts along dimension 0, may hold values from -0.109375 to 0.109375
- master_norm: float32 [1536], P(('shift', 'batch')), parts along dimension 0, may hold values from 0.25 to 1.75
- master_bias: float32 [1536], P(('shift', 'batch')), parts along dimension 0, may hold values from -3 to 3
- memory_up: float32 [1536, 3072], P(('shift', 'batch'), 'cols'), parts along dimension 0, may hold values from -1.75 to 1.75
- memory_down: float32 [6144, 768], P(('shift', 'cols'), 'batch'), parts along dimension 0, may hold values from -1.75 to 1.75
- memory_norm: float32 [1536], P(('shift', 'batch')), parts along dimension 0, may hold values from -1.75 to 1.75
- memory_bias: float32 [1536], P(('shift', 'batch')), parts along dimension 0, may hold values from -1.75 to 1.75
Outputs:
- compute_up: bfloat16 [1536, 3072], P('shift', 'cols'), parts along dimension 0
- compute_down: bfloat16 [6144, 768], P(('shift', 'cols')), parts along dimension 0
- compute_norm: bfloat16 [1536], P('shift'), parts along dimension 0
- compute_bias: bfloat16 [1536], P('shift'), parts along dimension 0
- stepped_up: float32 [1536, 3072], P(('shift', 'batch'), 'cols'), parts along dimension 0
- stepped_down: float32 [6144, 768], P(('shift', 'cols'), 'batch'), parts along dimension 0
- stepped_norm: float32 [1536], P(('shift', 'batch')), parts along dimension 0
- stepped_bias: float32 [1536], P(('shift', 'batch')), parts along dimension 0
- state_new_up: float32 [1536, 3072], P(('shift', 'batch'), 'cols'), parts along dimension 0
- state_new_down: float32 [6144, 768], P(('shift', 'cols'), 'batch'), parts along dimension 0
- state_new_norm: float32 [1536], P(('shift', 'batch')), parts along dimension 0
- state_new_bias: float32 [1536], P(('shift', 'batch')), parts along dimension 0
There are 2 independent parts, one for each index of `shift`. A program takes and returns all parts, laid end to end along the dimension named above; each array names one. Nothing has to cross between parts.
All inputs are finite; a program needn't handle non-finite values.
Results may differ from a plain program's by a relative error of at most 0.0085.
Values may be sent and summed in bfloat16 or wider, within the bound.
A program may use at most 64 MiB of HBM per device.

v0:
```python
import jax
import jax.numpy as jnp
from jax import lax
from jax.sharding import PartitionSpec as P

learn_rate = 0.1
hold_rate = 0.8


def on_device(
    partial_up,
    partial_down,
    partial_norm,
    partial_bias,
    master_up,
    master_down,
    master_norm,
    master_bias,
    memory_up,
    memory_down,
    memory_norm,
    memory_bias,
):
    mean_up, mean_down = (
        lax.psum_scatter(
            partial_up[0].astype(jnp.bfloat16), "batch", scatter_dimension=0, tiled=True
        ).astype(jnp.float32),
        lax.psum_scatter(
            partial_down[0].astype(jnp.bfloat16), "batch", scatter_dimension=1, tiled=True
        ).astype(jnp.float32),
    )
    whole_norm, whole_bias = lax.psum((partial_norm[0], partial_bias[0]), "batch")
    place = lax.axis_index("batch")
    mean_norm = lax.dynamic_slice_in_dim(
        whole_norm, place * master_norm.shape[0], master_norm.shape[0]
    )
    mean_bias = lax.dynamic_slice_in_dim(
        whole_bias, place * master_bias.shape[0], master_bias.shape[0]
    )
    mean_rate = lax.axis_size("batch") ** (-0.5)
    mean_up = mean_up * mean_rate
    mean_down = mean_down * mean_rate
    mean_norm = mean_norm * mean_rate
    mean_bias = mean_bias * mean_rate
    state_new_up = hold_rate * memory_up + mean_up
    stepped_up = master_up - learn_rate * state_new_up
    state_new_down = hold_rate * memory_down + mean_down
    stepped_down = master_down - learn_rate * state_new_down
    state_new_norm = hold_rate * memory_norm + mean_norm
    stepped_norm = master_norm - learn_rate * state_new_norm
    state_new_bias = hold_rate * memory_bias + mean_bias
    stepped_bias = master_bias - learn_rate * state_new_bias
    compute_up, compute_down, compute_norm, compute_bias = (
        lax.all_gather(stepped_up.astype(jnp.bfloat16), "batch", axis=0, tiled=True),
        lax.all_gather(stepped_down.astype(jnp.bfloat16), "batch", axis=1, tiled=True),
        lax.all_gather(stepped_norm.astype(jnp.bfloat16), "batch", axis=0, tiled=True),
        lax.all_gather(stepped_bias.astype(jnp.bfloat16), "batch", axis=0, tiled=True),
    )
    return (
        compute_up,
        compute_down,
        compute_norm,
        compute_bias,
        stepped_up,
        stepped_down,
        stepped_norm,
        stepped_bias,
        state_new_up,
        state_new_down,
        state_new_norm,
        state_new_bias,
    )


def solution(mesh):
    return jax.shard_map(
        on_device,
        mesh=mesh,
        in_specs=(
            P(("shift", "batch"), None, "cols"),
            P(("shift", "batch"), "cols", None),
            P(("shift", "batch"), None),
            P(("shift", "batch"), None),
            P(("shift", "batch"), "cols"),
            P(("shift", "cols"), "batch"),
            P(("shift", "batch")),
            P(("shift", "batch")),
            P(("shift", "batch"), "cols"),
            P(("shift", "cols"), "batch"),
            P(("shift", "batch")),
            P(("shift", "batch")),
        ),
        out_specs=(
            P("shift", "cols"),
            P(("shift", "cols"), None),
            P("shift"),
            P("shift"),
            P(("shift", "batch"), "cols"),
            P(("shift", "cols"), "batch"),
            P(("shift", "batch")),
            P(("shift", "batch")),
            P(("shift", "batch"), "cols"),
            P(("shift", "cols"), "batch"),
            P(("shift", "batch")),
            P(("shift", "batch")),
        ),
        check_vma=False,
    )
```

profile of v0, /device:TPU:0, one launch (start us, length us, event | category | flops | bytes accessed | tf_op | source)
XLA Modules:
  0.0 146.6 jit_solution(9095668395752551022)
XLA Ops:
  7.2 0.0 reduce-scatter.3.cloned.1.call-start
  7.2 2.9 %convert_bitcast_fusion.1 = bf16[768,768]{1,0:T(8,128)(2,1)} fusion(f32[1,768,768]{2,1,0:T(8,128)} %param.12), kind=kLoop, calls=%fused_computation.1 | loop fusion | flops 589824 | bytes 3538944 | tf_op jit(solution)/shard_map/convert_element_type | solution.py:26
  10.2 0.0 reduce-scatter.3.cloned.1.call-update
  10.2 0.0 reduce-scatter.5.cloned.1.call-start
  10.3 1.5 %copy.24 = bf16[1,768,768]{1,2,0:T(8,128)(2,1)} copy(f32[1,768,768]{2,1,0:T(8,128)S(1)} %copy-done) | data formatting | bytes 3538944 | tf_op args[1]
  11.8 0.0 reduce-scatter.5.cloned.1.call-update
  11.8 0.0 all-gather.3.cloned.1.call-start
  11.8 31.1 %reduce-scatter.3.cloned.1.call-done = bf16[192,768]{1,0:T(8,128)(2,1)} async-done(((bf16[768,768]{1,0:T(8,128)(2,1)}), bf16[192,768]{1,0:T(8,128)(2,1)}) %reduce-scatter.3.cloned.1.call-update) | async-done | bytes 294928 | tf_op jit(solution)/shard_map/reduce_scatter | solution.py:25
  43.0 2.2 %fusion.3 = (bf16[192,768]{1,0:T(8,128)(2,1)}, f32[192,768]{1,0:T(8,128)}, f32[192,768]{1,0:T(8,128)}) fusion(f32[192,768]{1,0:T(8,128)S(1)} %copy-done.2, bf16[192,768]{1,0:T(8,128)(2,1)} %reduce-scatter.3.cloned.1.call-done, f32[192,768]{1,0:T(8,128)S(1)} %copy-done.3), kind=kLoop, calls=%fused_computation.13 | loop fusion | flops 1032192 | bytes 2949120 | tf_op jit(solution)/shard_map/convert_element_type | solution.py:54
  45.1 0.0 all-gather.3.cloned.1.call-update
  45.3 0.0 all-gather.5.cloned.1.call-start
  45.3 28.5 %reduce-scatter.5.cloned.1.call-done = bf16[768,192]{0,1:T(8,128)(2,1)} async-done(((bf16[768,768]{0,1:T(8,128)(2,1)}), bf16[768,192]{0,1:T(8,128)(2,1)}) %reduce-scatter.5.cloned.1.call-update) | async-done | bytes 294928 | tf_op jit(solution)/shard_map/reduce_scatter | solution.py:28
  73.8 2.2 %fusion.2 = (bf16[768,192]{0,1:T(8,128)(2,1)}, f32[768,192]{0,1:T(8,128)}, f32[768,192]{0,1:T(8,128)}) fusion(f32[768,192]{0,1:T(8,128)S(1)} %copy-done.4, bf16[768,192]{0,1:T(8,128)(2,1)} %reduce-scatter.5.cloned.1.call-done, f32[768,192]{0,1:T(8,128)S(1)} %copy-done.5), kind=kLoop, calls=%fused_computation.12 | loop fusion | flops 1032192 | bytes 2949120 | tf_op jit(solution)/shard_map/convert_element_type | solution.py:55
  76.0 0.0 all-gather.5.cloned.1.call-update
  76.1 0.6 dynamic-slice
  77.3 9.6 %all-reduce.2 = (f32[768]{0:T(1024)S(1)}, f32[768]{0:T(1024)S(1)}) all-reduce(f32[768]{0:T(1024)S(1)} %reduce, f32[768]{0:T(1024)S(1)} %reduce.1), channel_id=1, replica_groups=mesh['shift'=2,'batch'=4,'cols'=4] {'batch'}, use_global_device_ids=true, to_apply=%region_2.0 | all-reduce | flops 1536 | bytes 12288 | tf_op jit(solution)/shard_map/psum | solution.py:32
  87.0 0.7 fusion
  87.7 0.2 dynamic-update-slice
  87.9 0.2 dynamic-update-slice.1
  88.1 10.7 %all-reduce.3 = (bf16[768]{0:T(1024)(128)(2,1)}, bf16[768]{0:T(1024)(128)(2,1)}) all-reduce(bf16[768]{0:T(1024)(128)(2,1)S(1)} %dynamic-update-slice, bf16[768]{0:T(1024)(128)(2,1)S(1)} %dynamic-update-slice.1), channel_id=1, replica_groups=mesh['shift'=2,'batch'=4,'cols'=4] {'batch'}, use_global_device_ids=true, to_apply=%add | all-reduce | flops 1536 | bytes 6144
  98.7 6.6 %all-gather.3.cloned.1.call-done = bf16[768,768]{1,0:T(8,128)(2,1)} async-done(((bf16[192,768]{1,0:T(8,128)(2,1)}), bf16[768,768]{1,0:T(8,128)(2,1)}) %all-gather.3.cloned.1.call-update) | async-done | bytes 1179664 | tf_op jit(solution)/shard_map/all_gather | solution.py:54
  105.3 31.4 %all-gather.5.cloned.1.call-done = bf16[768,768]{0,1:T(8,128)(2,1)} async-done(((bf16[768,192]{0,1:T(8,128)(2,1)}), bf16[768,768]{0,1:T(8,128)(2,1)}) %all-gather.5.cloned.1.call-update) | async-done | bytes 1179664 | tf_op jit(solution)/shard_map/all_gather | solution.py:55
  136.7 2.4 %copy.25 = bf16[768,768]{1,0:T(8,128)(2,1)} copy(bf16[768,768]{0,1:T(8,128)(2,1)} %all-gather.5.cloned.1.call-done) | data formatting | bytes 2359296
  139.1 1.0 copy.29
  (30 shorter events, 0.1 us)
Async XLA Ops:
  7.2 35.8 %reduce-scatter.3.cloned.1.call-start = ((), (), s32[]{:S(2)}) async-start(), calls=%async_computation.2 | async-start | bytes 1474560 | tf_op jit(solution)/shard_map/reduce_scatter | solution.py:25
  7.2 3.0 %copy-start = (f32[1,768,768]{2,1,0:T(8,128)S(1)}, f32[1,768,768]{2,1,0:T(8,128)}, u32[]{:S(2)}) copy-start(f32[1,768,768]{2,1,0:T(8,128)} %param.13) | copy-start | bytes 7077892
  10.2 63.6 %reduce-scatter.5.cloned.1.call-start = ((), (), s32[]{:S(2)}) async-start(), calls=%async_computation.4 | async-start | bytes 1474560 | tf_op jit(solution)/shard_map/reduce_scatter | solution.py:28
  11.7 31.2 %copy-start.2 = (f32[192,768]{1,0:T(8,128)S(1)}, f32[192,768]{1,0:T(8,128)}, u32[]{:S(2)}) copy-start(f32[192,768]{1,0:T(8,128)} %param.16) | copy-start | bytes 1769476
  11.7 31.2 %copy-start.3 = (f32[192,768]{1,0:T(8,128)S(1)}, f32[192,768]{1,0:T(8,128)}, u32[]{:S(2)}) copy-start(f32[192,768]{1,0:T(8,128)} %param.20) | copy-start | bytes 1769476
  11.8 62.0 %copy-start.4 = (f32[768,192]{0,1:T(8,128)S(1)}, f32[768,192]{0,1:T(8,128)}, u32[]{:S(2)}) copy-start(f32[768,192]{0,1:T(8,128)} %param.17) | copy-start | bytes 1769476
  11.8 62.0 %copy-start.5 = (f32[768,192]{0,1:T(8,128)S(1)}, f32[768,192]{0,1:T(8,128)}, u32[]{:S(2)}) copy-start(f32[768,192]{0,1:T(8,128)} %param.21) | copy-start | bytes 1769476
  11.8 93.5 %all-gather.3.cloned.1.call-start = ((), (), s32[]{:S(2)}) async-start(), calls=%async_computation.3 | async-start | bytes 1474560 | tf_op jit(solution)/shard_map/all_gather | solution.py:54
  45.2 30.9 %copy-start.6 = (f32[1,768]{1,0:T(1,128)S(1)}, f32[1,768]{1,0:T(1,128)}, u32[]{:S(2)}) copy-start(f32[1,768]{1,0:T(1,128)} %param.14) | copy-start | bytes 9220
  45.2 30.9 %copy-start.7 = (f32[1,768]{1,0:T(1,128)S(1)}, f32[1,768]{1,0:T(1,128)}, u32[]{:S(2)}) copy-start(f32[1,768]{1,0:T(1,128)} %param.15) | copy-start | bytes 9220
  45.2 30.9 %copy-start.12 = (u32[32]{0:T(128)S(1)}, u32[32]{0:T(128)}, u32[]{:S(2)}) copy-start(u32[32]{0:T(128)} %constant.29) | copy-start | bytes 388
  45.2 41.8 %copy-start.8 = (f32[192]{0:T(256)S(1)}, f32[192]{0:T(256)}, u32[]{:S(2)}) copy-start(f32[192]{0:T(256)} %param.19) | copy-start | bytes 2308
  45.2 41.8 %copy-start.9 = (f32[192]{0:T(256)S(1)}, f32[192]{0:T(256)}, u32[]{:S(2)}) copy-start(f32[192]{0:T(256)} %param.23) | copy-start | bytes 2308
  45.2 41.8 %copy-start.10 = (f32[192]{0:T(256)S(1)}, f32[192]{0:T(256)}, u32[]{:S(2)}) copy-start(f32[192]{0:T(256)} %param.18) | copy-start | bytes 2308
  45.2 41.8 %copy-start.11 = (f32[192]{0:T(256)S(1)}, f32[192]{0:T(256)}, u32[]{:S(2)}) copy-start(f32[192]{0:T(256)} %param.22) | copy-start | bytes 2308
  45.3 91.5 %all-gather.5.cloned.1.call-start = ((), (), s32[]{:S(2)}) async-start(), calls=%async_computation.5 | async-start | bytes 1474560 | tf_op jit(solution)/shard_map/all_gather | solution.py:55
  105.3 33.8 %copy-start.1 = (bf16[768,768]{1,0:T(8,128)(2,1)S(1)}, bf16[768,768]{1,0:T(8,128)(2,1)}, u32[]{:S(2)}) copy-start(bf16[768,768]{1,0:T(8,128)(2,1)} %all-gather.3.cloned.1.call-done) | copy-start | bytes 3538948
Sparse Core Ops, SparseCore 0:
  10.9 32.0 reduce-scatter.2
  45.8 27.9 reduce-scatter.4
  75.9 29.3 all-gather.2
  107.3 29.3 all-gather.4
where the time goes:
time: 147 us
  waiting for transfers between devices  97.6 us (66%)
  blocking collectives  20.3 us (14%)
  between operations  14.6 us (10%)
  other arithmetic  8.02 us (5%)
  local copies, waits for them, and re-layouts  5.93 us (4%)
    all_gather x1, waiting for transfers between devices, on_device(): lax.all_gather(stepped_down.astype(jnp.bfloat16), 'batch', axis=1, tiled=...  31.4 us
    reduce_scatter x1, waiting for transfers between devices, on_device(): lax.psum_scatter(partial_up[0].astype(jnp.bfloat16), 'batch', scatter_dim...  31.1 us
    reduce_scatter x1, waiting for transfers between devices, on_device(): lax.psum_scatter(partial_down[0].astype(jnp.bfloat16), 'batch', scatter_d...  28.5 us
    unnamed x1, blocking collectives  10.7 us
    psum x1, blocking collectives, on_device(): lax.psum((partial_norm[0], partial_bias[0]), 'batch')  9.62 us
    all_gather x1, waiting for transfers between devices, on_device(): lax.all_gather(stepped_up.astype(jnp.bfloat16), 'batch', axis=0, tiled=True)  6.57 us
    unnamed x34, local copies, waits for them, and re-layouts  5.93 us
    convert_element_type x1, other arithmetic, on_device(): partial_up[0].astype(jnp.bfloat16)  2.94 us
  transfers between devices with their start and end apart: 4, of which 4 were waited for; matrix products, arithmetic and copies ran while one was open for 5% of the time, Pallas kernels for 0%

commit v1 on v0

--- a/solution.py
+++ b/solution.py
@@ -52,7 +52,7 @@
     stepped_bias = master_bias - learn_rate * state_new_bias
     compute_up, compute_down, compute_norm, compute_bias = (
         lax.all_gather(stepped_up.astype(jnp.bfloat16), "batch", axis=0, tiled=True),
-        lax.all_gather(stepped_down.astype(jnp.bfloat16), "batch", axis=1, tiled=True),
+        jnp.concatenate(lax.all_gather(stepped_down.astype(jnp.bfloat16), "batch"), axis=1),
         lax.all_gather(stepped_norm.astype(jnp.bfloat16), "batch", axis=0, tiled=True),
         lax.all_gather(stepped_bias.astype(jnp.bfloat16), "batch", axis=0, tiled=True),
     )

time: 147 us -> 145 us (0.986)
  waiting for transfers between devices: 97.6 us -> 93 us
  local copies, waits for them, and re-layouts: 5.93 us -> 10.5 us
  other arithmetic: 8.02 us -> 6.2 us
    all_gather x1, waiting for transfers between devices: 31.4 us -> 5.67 us  [on_device(): lax.all_gather(stepped_down.astype(jnp.bfloat16), 'batch')]
    all_gather x1, waiting for transfers between devices: 6.57 us -> 27.2 us  [on_device(): lax.all_gather(stepped_up.astype(jnp.bfloat16), 'batch', axis=0, tiled=True)]
    reduce_scatter x1, waiting for transfers between devices: 28.5 us -> 31.6 us  [on_device(): lax.psum_scatter(partial_down[0].astype(jnp.bfloat16), 'batch', scatter_d...]
    all_gather x0 -> x1, local copies, waits for them, and re-layouts: none -> 2.7 us  [on_device(): lax.all_gather(stepped_down.astype(jnp.bfloat16), 'batch')]
    reduce_scatter x1, waiting for transfers between devices: 31.1 us -> 28.5 us  [on_device(): lax.psum_scatter(partial_up[0].astype(jnp.bfloat16), 'batch', scatter_dim...]
    convert_element_type x1, other arithmetic: 2.94 us -> 1.13 us  [on_device(): partial_up[0].astype(jnp.bfloat16)]
    unnamed x34 -> x32, local copies, waits for them, and re-layouts: 5.93 us -> 7.7 us
  transfers between devices with their start and end apart: 4 -> 4, of which waited for: 4 -> 4; matrix products, arithmetic and copies ran while one was open for 5% -> 8% of each run, Pallas kernels for 0% -> 0%
where the time goes in v1:
time: 145 us
  waiting for transfers between devices  93 us (64%)
  blocking collectives  20.5 us (14%)
  between operations  14.6 us (10%)
  local copies, waits for them, and re-layouts  10.5 us (7%)
  other arithmetic  6.2 us (4%)
    reduce_scatter x1, waiting for transfers between devices, on_device(): lax.psum_scatter(partial_down[0].astype(jnp.bfloat16), 'batch', scatter_d...  31.6 us
    reduce_scatter x1, waiting for transfers between devices, on_device(): lax.psum_scatter(partial_up[0].astype(jnp.bfloat16), 'batch', scatter_dim...  28.5 us
    all_gather x1, waiting for transfers between devices, on_device(): lax.all_gather(stepped_up.astype(jnp.bfloat16), 'batch', axis=0, tiled=True)  27.2 us
    unnamed x1, blocking collectives  10.9 us
    psum x1, blocking collectives, on_device(): lax.psum((partial_norm[0], partial_bias[0]), 'batch')  9.62 us
    unnamed x32, local copies, waits for them, and re-layouts  7.7 us
    all_gather x1, waiting for transfers between devices, on_device(): lax.all_gather(stepped_down.astype(jnp.bfloat16), 'batch')  5.67 us
  transfers between devices with their start and end apart: 4, of which 4 were waited for; matrix products, arithmetic and copies ran while one was open for 8% of the time, Pallas kernels for 0%

profile of v1, /device:TPU:0, one launch (start us, length us, event | category | flops | bytes accessed | tf_op | source)
XLA Modules:
  0.0 145.0 jit_solution(15452401014706036250)
XLA Ops:
  7.2 0.0 reduce-scatter.5.cloned.1.call-start
  7.2 2.8 %copy.28 = bf16[1,768,768]{1,2,0:T(8,128)(2,1)} copy(f32[1,768,768]{2,1,0:T(8,128)} %param.13) | data formatting | bytes 3538944 | tf_op args[1]
  10.1 0.0 reduce-scatter.3.cloned.1.call-start
  10.2 1.1 convert_bitcast_fusion.1
  11.3 0.0 reduce-scatter.3.cloned.1.call-update
  11.3 0.0 all-gather.6.cloned.1.call-start
  11.4 31.6 %reduce-scatter.5.cloned.1.call-done = bf16[768,192]{0,1:T(8,128)(2,1)} async-done(((bf16[768,768]{0,1:T(8,128)(2,1)}), bf16[768,192]{0,1:T(8,128)(2,1)}) %reduce-scatter.5.cloned.1.call-update) | async-done | bytes 294928 | tf_op jit(solution)/shard_map/reduce_scatter | solution.py:28
  42.9 2.2 %fusion.2 = (bf16[768,192]{0,1:T(8,128)(2,1)}, f32[768,192]{0,1:T(8,128)}, f32[768,192]{0,1:T(8,128)}) fusion(f32[768,192]{0,1:T(8,128)S(1)} %copy-done.1, bf16[768,192]{0,1:T(8,128)(2,1)} %reduce-scatter.5.cloned.1.call-done, f32[768,192]{0,1:T(8,128)S(1)} %copy-done.2), kind=kLoop, calls=%fused_computation.12 | loop fusion | flops 1032192 | bytes 2949120 | tf_op jit(solution)/shard_map/convert_element_type | solution.py:55
  45.1 0.0 all-gather.6.cloned.1.call-update
  45.2 0.0 all-gather.4.cloned.1.call-start
  45.3 28.5 %reduce-scatter.3.cloned.1.call-done = bf16[192,768]{1,0:T(8,128)(2,1)} async-done(((bf16[768,768]{1,0:T(8,128)(2,1)}), bf16[192,768]{1,0:T(8,128)(2,1)}) %reduce-scatter.3.cloned.1.call-update) | async-done | bytes 294928 | tf_op jit(solution)/shard_map/reduce_scatter | solution.py:25
  73.8 2.2 %fusion.3 = (bf16[192,768]{1,0:T(8,128)(2,1)}, f32[192,768]{1,0:T(8,128)}, f32[192,768]{1,0:T(8,128)}) fusion(f32[192,768]{1,0:T(8,128)S(1)} %copy-done.3, bf16[192,768]{1,0:T(8,128)(2,1)} %reduce-scatter.3.cloned.1.call-done, f32[192,768]{1,0:T(8,128)S(1)} %copy-done.4), kind=kLoop, calls=%fused_computation.13 | loop fusion | flops 1032192 | bytes 2949120 | tf_op jit(solution)/shard_map/convert_element_type | solution.py:54
  76.1 0.6 dynamic-slice
  77.3 9.6 %all-reduce.2 = (f32[768]{0:T(1024)S(1)}, f32[768]{0:T(1024)S(1)}) all-reduce(f32[768]{0:T(1024)S(1)} %reduce, f32[768]{0:T(1024)S(1)} %reduce.1), channel_id=1, replica_groups=mesh['shift'=2,'batch'=4,'cols'=4] {'batch'}, use_global_device_ids=true, to_apply=%region_2.0 | all-reduce | flops 1536 | bytes 12288 | tf_op jit(solution)/shard_map/psum | solution.py:32
  87.0 0.7 fusion
  87.7 0.2 dynamic-update-slice
  87.9 0.2 dynamic-update-slice.1
  88.1 10.9 %all-reduce.3 = (bf16[768]{0:T(1024)(128)(2,1)}, bf16[768]{0:T(1024)(128)(2,1)}) all-reduce(bf16[768]{0:T(1024)(128)(2,1)S(1)} %dynamic-update-slice, bf16[768]{0:T(1024)(128)(2,1)S(1)} %dynamic-update-slice.1), channel_id=1, replica_groups=mesh['shift'=2,'batch'=4,'cols'=4] {'batch'}, use_global_device_ids=true, to_apply=%add | all-reduce | flops 1536 | bytes 6144
  99.0 5.7 %all-gather.6.cloned.1.call-done = bf16[3072,192]{0,1:T(8,128)(2,1)} async-done(((bf16[768,192]{0,1:T(8,128)(2,1)}), bf16[3072,192]{0,1:T(8,128)(2,1)}) %all-gather.6.cloned.1.call-update) | async-done | bytes 1179664 | tf_op jit(solution)/shard_map/all_gather | solution.py:55
  104.6 2.7 %reshape.34 = bf16[4,768,192]{1,0,2:T(4,128)(2,1)S(1)} reshape(bf16[3072,192]{0,1:T(8,128)(2,1)} %all-gather.6.cloned.1.call-done) | data formatting | bytes 2359296 | tf_op jit(solution)/shard_map/all_gather | solution.py:55
  107.3 0.1 copy.29
  107.5 1.5 %copy.30 = bf16[768,768]{1,0:T(8,128)(2,1)} copy(bf16[768,768]{0,1:T(8,128)(2,1)S(1)} %bitcast.12) | data formatting | bytes 2359296
  108.9 27.2 %all-gather.4.cloned.1.call-done = bf16[768,768]{1,0:T(8,128)(2,1)} async-done(((bf16[192,768]{1,0:T(8,128)(2,1)}), bf16[768,768]{1,0:T(8,128)(2,1)}) %all-gather.4.cloned.1.call-update) | async-done | bytes 1179664 | tf_op jit(solution)/shard_map/all_gather | solution.py:54
  136.1 2.4 %copy.34 = bf16[768,768]{1,0:T(8,128)(2,1)} copy(bf16[768,768]{1,0:T(8,128)(2,1)} %all-gather.4.cloned.1.call-done) | data formatting | bytes 2359296
  (30 shorter events, 0.1 us)
Async XLA Ops:
  7.2 35.8 %reduce-scatter.5.cloned.1.call-start = ((), (), s32[]{:S(2)}) async-start(), calls=%async_computation.4 | async-start | bytes 1474560 | tf_op jit(solution)/shard_map/reduce_scatter | solution.py:28
  7.2 2.9 %copy-start = (f32[1,768,768]{2,1,0:T(8,128)S(1)}, f32[1,768,768]{2,1,0:T(8,128)}, u32[]{:S(2)}) copy-start(f32[1,768,768]{2,1,0:T(8,128)} %param.12) | copy-start | bytes 7077892
  10.1 63.7 %reduce-scatter.3.cloned.1.call-start = ((), (), s32[]{:S(2)}) async-start(), calls=%async_computation.2 | async-start | bytes 1474560 | tf_op jit(solution)/shard_map/reduce_scatter | solution.py:25
  11.3 31.7 %copy-start.1 = (f32[768,192]{0,1:T(8,128)S(1)}, f32[768,192]{0,1:T(8,128)}, u32[]{:S(2)}) copy-start(f32[768,192]{0,1:T(8,128)} %param.17) | copy-start | bytes 1769476
  11.3 31.7 %copy-start.2 = (f32[768,192]{0,1:T(8,128)S(1)}, f32[768,192]{0,1:T(8,128)}, u32[]{:S(2)}) copy-start(f32[768,192]{0,1:T(8,128)} %param.21) | copy-start | bytes 1769476
  11.3 62.5 %copy-start.3 = (f32[192,768]{1,0:T(8,128)S(1)}, f32[192,768]{1,0:T(8,128)}, u32[]{:S(2)}) copy-start(f32[192,768]{1,0:T(8,128)} %param.16) | copy-start | bytes 1769476
  11.3 62.5 %copy-start.4 = (f32[192,768]{1,0:T(8,128)S(1)}, f32[192,768]{1,0:T(8,128)}, u32[]{:S(2)}) copy-start(f32[192,768]{1,0:T(8,128)} %param.20) | copy-start | bytes 1769476
  11.3 93.3 %all-gather.6.cloned.1.call-start = ((), (), s32[]{:S(2)}) async-start(), calls=%async_computation.5 | async-start | bytes 1474560 | tf_op jit(solution)/shard_map/all_gather | solution.py:55
  45.2 30.9 %copy-start.5 = (f32[1,768]{1,0:T(1,128)S(1)}, f32[1,768]{1,0:T(1,128)}, u32[]{:S(2)}) copy-start(f32[1,768]{1,0:T(1,128)} %param.14) | copy-start | bytes 9220
  45.2 30.9 %copy-start.6 = (f32[1,768]{1,0:T(1,128)S(1)}, f32[1,768]{1,0:T(1,128)}, u32[]{:S(2)}) copy-start(f32[1,768]{1,0:T(1,128)} %param.15) | copy-start | bytes 9220
  45.2 30.9 %copy-start.11 = (u32[32]{0:T(128)S(1)}, u32[32]{0:T(128)}, u32[]{:S(2)}) copy-start(u32[32]{0:T(128)} %constant.29) | copy-start | bytes 388
  45.2 41.8 %copy-start.7 = (f32[192]{0:T(256)S(1)}, f32[192]{0:T(256)}, u32[]{:S(2)}) copy-start(f32[192]{0:T(256)} %param.19) | copy-start | bytes 2308
  45.2 41.8 %copy-start.8 = (f32[192]{0:T(256)S(1)}, f32[192]{0:T(256)}, u32[]{:S(2)}) copy-start(f32[192]{0:T(256)} %param.23) | copy-start | bytes 2308
  45.2 41.8 %copy-start.9 = (f32[192]{0:T(256)S(1)}, f32[192]{0:T(256)}, u32[]{:S(2)}) copy-start(f32[192]{0:T(256)} %param.18) | copy-start | bytes 2308
  45.2 41.8 %copy-start.10 = (f32[192]{0:T(256)S(1)}, f32[192]{0:T(256)}, u32[]{:S(2)}) copy-start(f32[192]{0:T(256)} %param.22) | copy-start | bytes 2308
  45.2 90.9 %all-gather.4.cloned.1.call-start = ((), (), s32[]{:S(2)}) async-start(), calls=%async_computation.3 | async-start | bytes 1474560 | tf_op jit(solution)/shard_map/all_gather | solution.py:54
Sparse Core Ops, SparseCore 0:
  10.9 32.0 reduce-scatter.4
  45.8 27.9 reduce-scatter.2
  75.4 29.2 all-gather.5
  106.6 29.4 all-gather.3
